TPU v7x, 256 devices: a whole 4x4x8 slice. The times are simulated.
256 devices in a mesh: rows: 64 (over x_hi, z, y), cols: 4 (over x_lo, core).
Axes of the slice: x: 4 (x_hi: 2, x_lo: 2; x = x_hi * 2 + x_lo), y: 4, z: 8, core: 2. Of those that a mesh axis runs over, the one named last changes fastest.
Arguments:
- tokens: bfloat16 [768, 96, 768], P('rows', 'cols'), may hold values from -48 to 48
- ln_gain: float32 [768], replicated, may hold values from 0.5 to 1.5
- ln_bias: float32 [768], replicated, may hold values from -3 to 3
- qkv_weight: bfloat16 [768, 2304], replicated, may hold values from -3 to 3
- qkv_bias: float32 [2304], replicated, may hold values from -3 to 3
- rel_table: float32 [23, 23, 24], replicated, may hold values from -4 to 4
- proj_weight: bfloat16 [768, 768], replicated, may hold values from -0.21875 to 0.21875
- proj_bias: float32 [768], replicated, may hold values from -3 to 3
- branch_weight: bfloat16 [4, 768, 512], replicated, may hold values from -0.21875 to 0.21875
- branch_bias: float32 [4, 512], replicated, may hold values from -4 to 4
- join_block: bfloat16 [768, 512], replicated, may hold values from -0.109375 to 0.109375
- join_branch: bfloat16 [4, 512, 512], replicated, may hold values from -0.375 to 0.375
- bn_gain: float32 [512], replicated, may hold values from 0.25 to 1.75
- bn_bias: float32 [512], replicated, may hold values from -4 to 4
Outputs:
- joined: bfloat16 [768, 96, 512], P('rows', 'cols')
All inputs are finite; a program needn't handle non-finite values.
Results may differ from a plain program's by a relative error of at most 0.0049.
Values may be sent and summed in bfloat16 or wider, within the bound.
A program may use at most 128 MiB of HBM per device.

v0:
```python
import jax
import jax.numpy as jnp
import numpy as np
from jax import lax
from jax.sharding import PartitionSpec as P

WIN = 12


bin_scales = (1, 2, 3, 6)
bin_starts = (0, 1, 3, 6)
norm_eps = 1e-05
highest = lax.Precision.HIGHEST


def passed_along(value, axis, steps):
    count = lax.axis_size(axis)
    pairs = [(source, (source + steps) % count) for source in range(count)]
    return lax.ppermute(value, axis, pairs)


def layer_norm(values, norm_gain, norm_bias):
    floats = values.astype(jnp.float32)
    center = jnp.mean(floats, -1, keepdims=True)
    spread_sq = jnp.mean(jnp.square(floats - center), -1, keepdims=True)
    return ((floats - center) * lax.rsqrt(spread_sq + norm_eps) * norm_gain + norm_bias).astype(
        jnp.bfloat16
    )


def relative_bias(rel_table):
    steps_idx = jnp.arange(WIN, dtype=jnp.int32)
    offsets = steps_idx[:, None] - steps_idx[None, :] + WIN - 1
    onehot = (
        offsets[:, :, None] == jnp.arange(2 * WIN - 1, dtype=jnp.int32)[None, None, :]
    ).astype(jnp.float32)
    pair_bias = jnp.einsum("pra,qsb,abh->hpqrs", onehot, onehot, rel_table, precision=highest)
    return pair_bias.reshape(rel_table.shape[2], WIN * WIN, WIN * WIN)


def region_labels(positions, total):
    return (positions >= total - WIN).astype(jnp.int32) + (positions >= total - WIN // 2).astype(
        jnp.int32
    )


def window_mask(row_place, col_place, height, breadth):
    labels = (
        3 * region_labels(row_place, height)[:, None] + region_labels(col_place, breadth)[None, :]
    )
    labels = labels.reshape(row_place.shape[0] // WIN, WIN, col_place.shape[0] // WIN, WIN)
    labels = labels.transpose(0, 2, 1, 3).reshape(-1, WIN * WIN)
    return jnp.where(labels[:, :, None] != labels[:, None, :], -100.0, 0.0).astype(jnp.float32)


def window_attention(normed, qkv_weight, qkv_bias, proj_weight, proj_bias, pair_bias, mask_add):
    row_count, col_count, width = normed.shape
    heads_count = pair_bias.shape[0]
    head_size = width // heads_count
    windows = normed.reshape(row_count // WIN, WIN, col_count // WIN, WIN, width)
    windows = windows.transpose(0, 2, 1, 3, 4).reshape(-1, WIN * WIN, width)
    count_win = windows.shape[0]
    mixed = (
        jnp.dot(windows.reshape(-1, width), qkv_weight, preferred_element_type=jnp.float32)
        + qkv_bias
    )
    mixed = mixed.reshape(count_win, WIN * WIN, 3, heads_count, head_size)
    queries = (mixed[:, :, 0] * head_size ** (-0.5)).astype(jnp.bfloat16)
    keys_bf = mixed[:, :, 1].astype(jnp.bfloat16)
    values_bf = mixed[:, :, 2].astype(jnp.bfloat16)
    scores = jnp.einsum("wihd,wjhd->whij", queries, keys_bf, preferred_element_type=jnp.float32)
    scores = scores + pair_bias[None] + mask_add[:, None]
    weights = jax.nn.softmax(scores, axis=-1).astype(jnp.bfloat16)
    context = jnp.einsum("whij,wjhd->wihd", weights, values_bf, preferred_element_type=jnp.float32)
    context = context.astype(jnp.bfloat16).reshape(-1, width)
    output = jnp.dot(context, proj_weight, preferred_element_type=jnp.float32) + proj_bias
    output = output.reshape(row_count // WIN, col_count // WIN, WIN, WIN, width).transpose(
        0, 2, 1, 3, 4
    )
    return output.reshape(row_count, col_count, width)


def bin_tables(positions, total):
    pooling = []
    spread = []
    place_f = positions.astype(jnp.float32)
    for scale_value in bin_scales:
        levels = jnp.arange(scale_value, dtype=jnp.int32)
        pooling.append(
            (positions[:, None] // (total // scale_value) == levels[None, :]).astype(jnp.float32)
        )
        source = jnp.clip((place_f + 0.5) * (scale_value / total) - 0.5, 0.0, scale_value - 1.0)
        spread.append(
            jax.nn.relu(1.0 - jnp.abs(source[:, None] - levels[None, :].astype(jnp.float32)))
        )
    return (jnp.concatenate(pooling, 1), jnp.concatenate(spread, 1))


def cell_selectors():
    row_select = np.zeros((12, 50), np.float32)
    col_select = np.zeros((12, 50), np.float32)
    column = 0
    for scale_value, start_value in zip(bin_scales, bin_starts):
        for upper in range(scale_value):
            for lower in range(scale_value):
                row_select[start_value + upper, column] = 1.0
                col_select[start_value + lower, column] = 1.0
                column += 1
    return (jnp.asarray(row_select, jnp.float32), jnp.asarray(col_select, jnp.float32))


def cell_counts(height, breadth):
    sizes_list = []
    for scale_value in bin_scales:
        sizes_list += [float(height // scale_value * (breadth // scale_value))] * (
            scale_value * scale_value
        )
    return jnp.asarray(sizes_list, jnp.float32)[:, None]


def local_pools(values, row_table, col_table):
    by_rows = jnp.einsum(
        "rk,rcd->kcd",
        row_table.astype(values.dtype),
        values,
        preferred_element_type=jnp.float32,
        precision=highest,
    )
    pieces = []
    for scale_value, start_value in zip(bin_scales, bin_starts):
        cell_block = jnp.einsum(
            "acd,cb->abd",
            by_rows[start_value : start_value + scale_value],
            col_table[:, start_value : start_value + scale_value],
            precision=highest,
        )
        pieces.append(cell_block.reshape(scale_value * scale_value, -1))
    return jnp.concatenate(pieces, 0)


def branch_projections(pooled, branch_weight, branch_bias, join_branch):
    results = []
    start_row = 0
    for branch_index, scale_value in enumerate(bin_scales):
        cell_rows = pooled[start_row : start_row + scale_value * scale_value]
        hidden_map = jax.nn.relu(
            jnp.dot(cell_rows, branch_weight[branch_index].astype(jnp.float32), precision=highest)
            + branch_bias[branch_index]
        )
        results.append(
            jnp.dot(hidden_map, join_branch[branch_index].astype(jnp.float32), precision=highest)
        )
        start_row += scale_value * scale_value
    return jnp.concatenate(results, 0)


def spread_cells(projected, row_spread, col_spread):
    total_map = jnp.zeros(
        (row_spread.shape[0], col_spread.shape[0], projected.shape[1]), jnp.float32
    )
    start_row = 0
    for scale_value, start_value in zip(bin_scales, bin_starts):
        block_cells = projected[start_row : start_row + scale_value * scale_value].reshape(
            scale_value, scale_value, -1
        )
        across = jnp.einsum(
            "cb,abh->ach",
            col_spread[:, start_value : start_value + scale_value],
            block_cells,
            precision=highest,
        )
        total_map = total_map + jnp.einsum(
            "ra,ach->rch",
            row_spread[:, start_value : start_value + scale_value],
            across,
            precision=highest,
        )
        start_row += scale_value * scale_value
    return total_map


def shards(
    tokens,
    ln_gain,
    ln_bias,
    qkv_weight,
    qkv_bias,
    rel_table,
    proj_weight,
    proj_bias,
    branch_weight,
    branch_bias,
    join_block,
    join_branch,
    bn_gain,
    bn_bias,
):
    row_count, col_count, width = tokens.shape
    height = row_count * lax.axis_size("rows")
    breadth = col_count * lax.axis_size("cols")
    half = WIN // 2
    upper_rows = passed_along(tokens[:half], "rows", -1)
    rolled_tok = jnp.concatenate([tokens[half:], upper_rows], 0)
    left_cols = passed_along(rolled_tok[:, :half], "cols", -1)
    rolled_tok = jnp.concatenate([rolled_tok[:, half:], left_cols], 1)
    row_place = lax.axis_index("rows") * row_count + jnp.arange(row_count, dtype=jnp.int32)
    col_place = lax.axis_index("cols") * col_count + jnp.arange(col_count, dtype=jnp.int32)
    normed = layer_norm(rolled_tok, ln_gain, ln_bias)
    mask_add = window_mask(row_place, col_place, height, breadth)
    attended = window_attention(
        normed, qkv_weight, qkv_bias, proj_weight, proj_bias, relative_bias(rel_table), mask_add
    )
    block_out = (rolled_tok.astype(jnp.float32) + attended).astype(jnp.bfloat16)
    row_orig = (row_place + half) % height
    col_orig = (col_place + half) % breadth
    row_pool, row_spread = bin_tables(row_orig, height)
    col_pool, col_spread = bin_tables(col_orig, breadth)
    counts = cell_counts(height, breadth)
    everyone = float(height * breadth)
    direct = jnp.dot(
        block_out.reshape(-1, width), join_block, preferred_element_type=jnp.float32
    ).reshape(row_count, col_count, -1)
    local_cells = local_pools(block_out, row_pool, col_pool)
    local_weighted = local_pools(direct, row_spread, col_spread)
    pooled, weighted, direct_sum, direct_squares = lax.psum(
        (
            local_cells,
            local_weighted,
            jnp.sum(direct, axis=(0, 1)),
            jnp.sum(jnp.square(direct), axis=(0, 1)),
        ),
        ("rows", "cols"),
    )
    projected = branch_projections(pooled / counts, branch_weight, branch_bias, join_branch)
    pre_norm = direct + spread_cells(projected, row_spread, col_spread)
    row_select, col_select = cell_selectors()
    full_rows = bin_tables(jnp.arange(height, dtype=jnp.int32), height)[1]
    full_cols = bin_tables(jnp.arange(breadth, dtype=jnp.int32), breadth)[1]
    gram_rows = jnp.dot(full_rows.T, full_rows, precision=highest)
    gram_cols = jnp.dot(full_cols.T, full_cols, precision=highest)
    gram_cells = jnp.dot(
        row_select.T, jnp.dot(gram_rows, row_select, precision=highest), precision=highest
    )
    gram_cells = gram_cells * jnp.dot(
        col_select.T, jnp.dot(gram_cols, col_select, precision=highest), precision=highest
    )
    cell_mass = jnp.dot(jnp.sum(full_rows, 0), row_select, precision=highest) * jnp.dot(
        jnp.sum(full_cols, 0), col_select, precision=highest
    )
    lifted_sum = jnp.dot(cell_mass, projected, precision=highest)
    lifted_squares = jnp.sum(projected * jnp.dot(gram_cells, projected, precision=highest), 0)
    cross_terms = jnp.sum(projected * weighted, 0)
    mean_val = (direct_sum + lifted_sum) / everyone
    variance = (direct_squares + 2.0 * cross_terms + lifted_squares) / everyone - jnp.square(
        mean_val
    )
    joined = jax.nn.relu(
        (pre_norm - mean_val) * lax.rsqrt(variance + norm_eps) * bn_gain + bn_bias
    ).astype(jnp.bfloat16)
    tail_cols = passed_along(joined[:, col_count - half :], "cols", 1)
    joined = jnp.concatenate([tail_cols, joined[:, : col_count - half]], 1)
    tail_rows = passed_along(joined[row_count - half :], "rows", 1)
    joined = jnp.concatenate([tail_rows, joined[: row_count - half]], 0)
    return joined


def solution(mesh):
    in_specs = (
        P("rows", "cols", None),
        P(),
        P(),
        P(),
        P(),
        P(),
        P(),
        P(),
        P(),
        P(),
        P(),
        P(),
        P(),
        P(),
    )
    out_specs = P("rows", "cols", None)
    return jax.shard_map(shards, mesh=mesh, in_specs=in_specs, out_specs=out_specs, check_vma=False)
```

profile of v0, /device:TPU:1, one launch (start us, length us, event | category | flops | bytes accessed | tf_op | source)
XLA Modules:
  0.0 452.4 jit_solution(9545579387952552729)
XLA Ops:
  6.5 2.0 fusion.182
  8.5 11.3 %collective-permute-start = (bf16[6,24,768]{2,1,0:T(8,128)(2,1)}, bf16[6,24,768]{2,1,0:T(8,128)(2,1)}, u32[]{:S(2)}, u32[]{:S(2)}) collective-permute-start(bf16[6,24,768]{2,1,0:T(8,128)(2,1)} %get-tuple-element.14), channel_id=1, source_target_pairs={{0,252},{4,0},{8,4},{12,8},{16,12},{20,16},{24,20},{28,24},{32,28}... | collective-permute-start | bytes 663560 | tf_op jit(solution)/shard_map/ppermute | solution.py:19
  31.8 1.3 add_bitcast_fusion
  33.9 0.8 compare_select_fusion
  34.7 2.0 convolution_bitcast_fusion.1
  36.8 8.9 %convolution_bitcast_fusion = f32[24,12,12,12,12]{0,4,2,3,1:T(8,128)} fusion(f32[23,24,12,12,1]{1,3,0,2,4:T(8,128)S(1)} %convolution_bitcast_fusion.1, s32[12,12]{1,0:T(8,128)S(1)} %subtract_add_fusion), kind=kOutput, calls=%fused_computation.1 | convolution fusion | flops 137358576 | bytes 2309184 | tf_op jit(solution)/shard_map/pra,qsb,abh->hpqrs/dot_general | solution.py:37
  45.6 12.3 %copy.59 = f32[24,12,12,12,12]{0,4,3,2,1:T(8,128)} copy(f32[24,12,12,12,12]{0,4,2,3,1:T(8,128)} %convolution_bitcast_fusion) | data formatting | bytes 3981312 | tf_op jit(solution)/shard_map/pra,qsb,abh->hpqrs/transpose | solution.py:37
  57.9 13.0 %add.642 = f32[24,144,144]{0,2,1:T(8,128)} reshape(f32[24,12,12,12,12]{0,4,3,2,1:T(8,128)} %copy.59) | data formatting | bytes 3981312 | tf_op jit(solution)/shard_map/add | solution.py:72
  70.9 12.6 %copy.60 = f32[24,144,144]{1,2,0:T(8,128)} copy(f32[24,144,144]{0,2,1:T(8,128)} %add.642) | data formatting | bytes 3981312 | tf_op jit(solution)/shard_map/add | solution.py:72
  83.5 1.3 subtract_maximum_fusion.7
  84.8 1.3 subtract_maximum_fusion.13
  86.1 1.3 subtract_maximum_fusion.16
  87.4 1.2 iota_compare_fusion.2
  88.6 1.2 iota_compare_fusion.4
  89.8 1.4 fusion.183
  93.4 1.4 convolution_bitcast_fusion.12
  94.7 0.8 fusion.185
  95.8 0.9 fusion.95
  96.8 0.9 convolution_multiply_fusion.1
  97.7 1.2 iota_compare_fusion.5
  98.9 0.9 pad_maximum_fusion.3
  99.8 1.2 collective-permute-start.1
  101.1 1.2 slice_maximum_fusion
  102.2 2.4 collective-permute-done.1
  106.0 1.4 multiply_reduce_fusion
  108.1 2.1 fusion.181
  110.2 2.3 reshape.627
  112.5 1.5 fusion.33
  114.1 0.9 copy.53
  114.9 1.9 reshape_reshape.3
  116.9 3.7 convolution_add_fusion
  120.6 2.4 copy.54
  123.0 5.1 %reshape.609 = f32[2,144,3,24,32]{1,0,4,3,2:T(2,128)} reshape(f32[288,2304]{0,1:T(8,128)S(1)} %copy.54) | data formatting | bytes 5308416 | tf_op jit(solution)/shard_map/reshape | solution.py:67
  128.1 2.8 copy.144
  131.0 0.9 copy-done.2
  132.6 4.0 fusion.18
  136.6 10.7 %fusion.184 = (f32[2,24,144]{2,1,0:T(8,128)S(1)}, f32[2,24,144,144]{2,3,1,0:T(8,128)}) fusion(f32[2,24,144,144]{2,3,1,0:T(8,128)} %fusion.18, f32[2,144,144]{1,2,0:T(8,128)S(1)} %copy-done.10, f32[24,144,144]{1,2,0:T(8,128)S(1)} %copy-done.3), kind=kOutput, calls=%fused_computation.308 | output fusion | flops 5972111 | bytes 10146816 | tf_op jit(solution)/shard_map/sub | solution.py:73
  147.3 3.8 fusion.8
  152.3 1.8 convolution_add_fusion.1
  154.4 1.0 reshape.612
  155.5 1.3 add_convert_fusion.1
  156.8 2.2 multiply_reduce_fusion.1
  159.0 1.1 fusion.26
  163.9 1.3 convolution_bitcast_fusion.8
  165.3 1.1 convolution_bitcast_fusion.10
  166.6 1.0 convolution_bitcast_fusion.4
  167.7 0.9 convolution_bitcast_fusion.7
  168.6 1.1 convolution_bitcast_fusion.9
  169.7 1.0 fusion.76
  174.3 72.7 %all-reduce = (f32[512]{0:T(512)}, f32[512]{0:T(512)}) all-reduce(f32[512]{0:T(512)} %get-tuple-element.6, f32[512]{0:T(512)} %get-tuple-element.5), channel_id=1, replica_groups=mesh['rows'=64,'cols'=4] {'rows','cols'}, use_global_device_ids=true, to_apply=%region_6.7 | all-reduce | flops 1024 | bytes 8192 | tf_op jit(solution)/shard_map/psum | solution.py:225
  247.0 165.2 %all-reduce.4.cloned.1.call-done = (f32[50,768]{1,0:T(8,128)}, f32[50,512]{1,0:T(8,128)}) async-done(((f32[50,768]{1,0:T(8,128)}, f32[50,512]{1,0:T(8,128)}), (f32[50,768]{1,0:T(8,128)}, f32[50,512]{1,0:T(8,128)})) %all-reduce.4.cloned.1.call-update) | async-done | bytes 256016 | tf_op jit(solution)/shard_map/psum | solution.py:225
  412.1 1.0 broadcast_multiply_fusion
  413.2 1.6 fusion.14
  414.8 1.6 fusion.9
  416.4 1.5 fusion.11
  418.7 1.6 fusion.12
  422.6 1.0 fusion.56
  424.1 1.7 fusion.63
  425.8 1.0 convolution_bitcast_fusion.5
  426.8 1.6 fusion.70
  429.8 2.2 fusion.40
  432.0 1.3 collective-permute-start.2
  433.3 1.6 collective-permute-done.2
  435.7 9.1 %collective-permute-done.3 = bf16[6,24,512]{2,1,0:T(8,128)(2,1)S(1)} collective-permute-done((bf16[6,24,512]{2,1,0:T(8,128)(2,1)S(1)}, bf16[6,24,512]{2,1,0:T(8,128)(2,1)S(1)}, u32[]{:S(2)}, u32[]{:S(2)}) %collective-permute-start.3) | collective-permute-done | bytes 147488 | tf_op jit(solution)/shard_map/ppermute | solution.py:19
  (170 shorter events, 33.5 us)
Async XLA Ops:
  6.5 110.3 %copy-start = (bf16[768,2304]{1,0:T(8,128)(2,1)S(1)}, bf16[768,2304]{1,0:T(8,128)(2,1)}, u32[]{:S(2)}) copy-start(bf16[768,2304]{1,0:T(8,128)(2,1)} %param.20) | copy-start | bytes 10616836
  6.5 405.6 %all-reduce.4.cloned.1.call-start = ((), (), s32[]{:S(2)}) async-start(), calls=%async_computation | async-start | bytes 573440 | tf_op jit(solution)/shard_map/psum | solution.py:225
  8.5 90.4 %collective-permute-start = (bf16[6,24,768]{2,1,0:T(8,128)(2,1)}, bf16[6,24,768]{2,1,0:T(8,128)(2,1)}, u32[]{:S(2)}, u32[]{:S(2)}) collective-permute-start(bf16[6,24,768]{2,1,0:T(8,128)(2,1)} %get-tuple-element.14), channel_id=1, source_target_pairs={{0,252},{4,0},{8,4},{12,8},{16,12},{20,16},{24,20},{28,24},{32,28}... | collective-permute-start | bytes 663560 | tf_op jit(solution)/shard_map/ppermute | solution.py:19
  21.0 10.8 %copy-start.17 = (f32[6]{0:T(128)}, f32[6]{0:T(128)S(1)}, u32[]{:S(2)}) copy-start(f32[6]{0:T(128)S(1)} %iota_convert_fusion) | copy-start | bytes 76
  21.0 24.7 %copy-start.19 = (f32[3]{0:T(128)}, f32[3]{0:T(128)S(1)}, u32[]{:S(2)}) copy-start(f32[3]{0:T(128)S(1)} %iota_convert_fusion.1) | copy-start | bytes 40
  70.9 22.5 %copy-start.13 = (f32[12,50]{1,0:T(8,128)S(1)}, f32[12,50]{1,0:T(8,128)}, u32[]{:S(2)}) copy-start(f32[12,50]{1,0:T(8,128)} %constant.264.clone) | copy-start | bytes 7204
  70.9 25.8 %copy-start.12 = (f32[12,50]{1,0:T(8,128)S(1)}, f32[12,50]{1,0:T(8,128)}, u32[]{:S(2)}) copy-start(f32[12,50]{1,0:T(8,128)} %constant.265.clone) | copy-start | bytes 7204
  91.9 7.9 %copy-start.14 = (f32[96,6]{0,1:T(8,128)}, f32[96,6]{0,1:T(8,128)S(1)}, u32[]{:S(2)}) copy-start(f32[96,6]{0,1:T(8,128)S(1)} %subtract_maximum_fusion.3) | copy-start | bytes 6916
  92.7 7.1 %copy-start.21 = (f32[96,3]{0,1:T(4,128)}, f32[96,3]{0,1:T(4,128)S(1)}, u32[]{:S(2)}) copy-start(f32[96,3]{0,1:T(4,128)S(1)} %subtract_maximum_fusion.9) | copy-start | bytes 3460
  93.4 6.4 %copy-start.24 = (f32[96,2]{0,1:T(2,128)}, f32[96,2]{0,1:T(2,128)S(1)}, u32[]{:S(2)}) copy-start(f32[96,2]{0,1:T(2,128)S(1)} %subtract_maximum_fusion.14) | copy-start | bytes 2308
  99.8 4.8 %collective-permute-start.1 = (bf16[12,6,768]{2,1,0:T(8,128)(2,1)S(1)}, bf16[12,6,768]{2,1,0:T(8,128)(2,1)S(1)}, u32[]{:S(2)}, u32[]{:S(2)}) collective-permute-start(bf16[12,6,768]{2,1,0:T(8,128)(2,1)S(1)} %pad_maximum_fusion.3), channel_id=1, source_target_pairs={{0,3},{1,0},{2,1},{3,2},{4,7},{5,4},{6,5},{7,6},{8,11},{9,8},{10,9... | collective-permute-start | bytes 331784 | tf_op jit(solution)/shard_map/ppermute | solution.py:19
  102.2 2.5 copy-start.4
  104.7 0.7 copy-start.7
  108.1 4.4 copy-start.28
  108.1 4.4 copy-start.29
  128.1 3.8 copy-start.2
  132.6 4.0 copy-start.3
  132.6 4.0 copy-start.10
  147.3 5.0 %copy-start.40 = (f32[768]{0:T(1024)S(1)}, f32[768]{0:T(1024)}, u32[]{:S(2)}) copy-start(f32[768]{0:T(1024)} %param.24) | copy-start | bytes 9220
  154.2 1.3 copy-start.5
  154.2 1.3 copy-start.8
  154.4 4.6 %copy-start.22 = (f32[12,6]{0,1:T(8,128)S(1)}, f32[12,6]{0,1:T(8,128)}, u32[]{:S(2)}) copy-start(f32[12,6]{0,1:T(8,128)} %subtract_maximum_fusion.7) | copy-start | bytes 868
  154.4 4.6 %copy-start.25 = (f32[12,3]{0,1:T(4,128)S(1)}, f32[12,3]{0,1:T(4,128)}, u32[]{:S(2)}) copy-start(f32[12,3]{0,1:T(4,128)} %subtract_maximum_fusion.13) | copy-start | bytes 436
  154.4 4.6 %copy-start.30 = (f32[12,2]{0,1:T(2,128)S(1)}, f32[12,2]{0,1:T(2,128)}, u32[]{:S(2)}) copy-start(f32[12,2]{0,1:T(2,128)} %subtract_maximum_fusion.16) | copy-start | bytes 292
  154.4 4.6 %copy-start.36 = (f32[12,1]{0,1:T(1,128)S(1)}, f32[12,1]{0,1:T(1,128)}, u32[]{:S(2)}) copy-start(f32[12,1]{0,1:T(1,128)} %subtract_maximum_fusion.20) | copy-start | bytes 148
  155.5 6.1 %copy-start.35 = (pred[12,6]{0,1:T(8,128)(4,1)S(1)}, pred[12,6]{0,1:T(8,128)(4,1)}, u32[]{:S(2)}) copy-start(pred[12,6]{0,1:T(8,128)(4,1)} %iota_compare_fusion.2) | copy-start | bytes 220
  155.5 6.1 %copy-start.37 = (pred[12,1]{0,1:T(4,128)(4,1)S(1)}, pred[12,1]{0,1:T(4,128)(4,1)}, u32[]{:S(2)}) copy-start(pred[12,1]{0,1:T(4,128)(4,1)} %fusion.146) | copy-start | bytes 40
  155.5 6.1 %copy-start.38 = (pred[12,3]{0,1:T(4,128)(4,1)S(1)}, pred[12,3]{0,1:T(4,128)(4,1)}, u32[]{:S(2)}) copy-start(pred[12,3]{0,1:T(4,128)(4,1)} %iota_compare_fusion.4) | copy-start | bytes 112
  155.5 6.1 %copy-start.39 = (pred[12,2]{0,1:T(4,128)(4,1)S(1)}, pred[12,2]{0,1:T(4,128)(4,1)}, u32[]{:S(2)}) copy-start(pred[12,2]{0,1:T(4,128)(4,1)} %iota_compare_fusion.5) | copy-start | bytes 76
  159.0 3.1 copy-start.6
  159.0 4.5 copy-start.18
  159.0 4.5 copy-start.32
  161.9 10.8 %copy-start.15 = (f32[96,6]{0,1:T(8,128)S(1)}, f32[96,6]{0,1:T(8,128)}, u32[]{:S(2)}) copy-start(f32[96,6]{0,1:T(8,128)} %copy-done.14) | copy-start | bytes 6916
  163.9 254.1 %copy-start.9 = (bf16[4,512,512]{2,1,0:T(8,128)(2,1)S(1)}, bf16[4,512,512]{2,1,0:T(8,128)(2,1)}, u32[]{:S(2)}) copy-start(bf16[4,512,512]{2,1,0:T(8,128)(2,1)} %param.28) | copy-start | bytes 6291460
  167.6 251.0 %copy-start.26 = (f32[1,512]{1,0:T(1,128)S(1)}, f32[1,512]{1,0:T(1,128)}, u32[]{:S(2)}) copy-start(f32[1,512]{1,0:T(1,128)} %get-tuple-element.15) | copy-start | bytes 6148
  413.1 8.6 %copy-start.11 = (f32[50,512]{1,0:T(8,128)S(1)}, f32[50,512]{1,0:T(8,128)}, u32[]{:S(2)}) copy-start(f32[50,512]{1,0:T(8,128)} %get-tuple-element.10) | copy-start | bytes 307204
  413.2 8.6 %copy-start.16 = (f32[50,50]{1,0:T(8,128)S(1)}, f32[50,50]{1,0:T(8,128)}, u32[]{:S(2)}) copy-start(f32[50,50]{1,0:T(8,128)} %convolution_multiply_fusion.1) | copy-start | bytes 30004
  414.7 7.3 %copy-start.33 = (f32[24]{0:T(128)S(1)}, f32[24]{0:T(128)}, u32[]{:S(2)}) copy-start(f32[24]{0:T(128)} %get-tuple-element.23) | copy-start | bytes 292
  414.7 7.9 %copy-start.34 = (f32[12]{0:T(128)S(1)}, f32[12]{0:T(128)}, u32[]{:S(2)}) copy-start(f32[12]{0:T(128)} %get-tuple-element.27) | copy-start | bytes 148
  416.4 7.3 %copy-start.20 = (f32[3]{0:T(128)S(1)}, f32[3]{0:T(128)}, u32[]{:S(2)}) copy-start(f32[3]{0:T(128)} %copy-done.19) | copy-start | bytes 40
  416.4 7.3 %copy-start.31 = (f32[24]{0:T(128)S(1)}, f32[24]{0:T(128)}, u32[]{:S(2)}) copy-start(f32[24]{0:T(128)} %get-tuple-element.24) | copy-start | bytes 292
  418.3 7.4 %copy-start.23 = (f32[2]{0:T(128)S(1)}, f32[2]{0:T(128)}, u32[]{:S(2)}) copy-start(f32[2]{0:T(128)} %iota_convert_fusion.2) | copy-start | bytes 28
  421.5 4.3 copy-start.27
  424.1 21.5 %copy-start.1 = (bf16[768,2304]{1,0:T(8,128)(2,1)S(1)}, bf16[768,2304]{1,0:T(8,128)(2,1)}, u32[]{:S(2)}) copy-start(bf16[768,2304]{1,0:T(8,128)(2,1)} %param.20) | copy-start | bytes 10616836
  432.0 2.9 collective-permute-start.2
  435.0 9.8 %collective-permute-start.3 = (bf16[6,24,512]{2,1,0:T(8,128)(2,1)S(1)}, bf16[6,24,512]{2,1,0:T(8,128)(2,1)S(1)}, u32[]{:S(2)}, u32[]{:S(2)}) collective-permute-start(bf16[6,24,512]{2,1,0:T(8,128)(2,1)S(1)} %fusion.65), channel_id=1, source_target_pairs={{0,4},{4,8},{8,12},{12,16},{16,20},{20,24},{24,28},{28,32},{32,36}... | collective-permute-start | bytes 442376 | tf_op jit(solution)/shard_map/ppermute | solution.py:19
Sparse Core Ops, SparseCore 0:
  172.2 239.8 all-reduce.3
where the time goes:
time: 456 us; the launch traced here: 452 us
  waiting for transfers between devices  178 us (39%)
  blocking collectives  72.7 us (16%)
  local copies, waits for them, and re-layouts  67.4 us (15%)
  matrix products  54.9 us (12%)
  other arithmetic  50.5 us (11%)
  starting transfers between devices  14.5 us (3%)
  between operations  14.1 us (3%)
    psum x1, waiting for transfers between devices, shards(): lax.psum((local_cells, local_weighted, jnp.sum(direct, axis=(0, 1)), jnp....  165 us
    psum x1, blocking collectives, shards(): lax.psum((local_cells, local_weighted, jnp.sum(direct, axis=(0, 1)), jnp....  72.7 us
    add x2, local copies, waits for them, and re-layouts, window_attention(): scores = scores + pair_bias[None] + mask_add[:, None]  25.6 us
    ppermute x4, starting transfers between devices, passed_along(): return lax.ppermute(value, axis, pairs)  14.5 us
    ppermute x4, waiting for transfers between devices, passed_along(): return lax.ppermute(value, axis, pairs)  13.2 us
    transpose x1, local copies, waits for them, and re-layouts, relative_bias(): jnp.einsum('pra,qsb,abh->hpqrs', onehot, onehot, rel_table, precision=hig...  12.3 us
    dot_general x2, matrix products, relative_bias(): jnp.einsum('pra,qsb,abh->hpqrs', onehot, onehot, rel_table, precision=hig...  10.9 us
    sub x1, other arithmetic, window_attention(): weights = jax.nn.softmax(scores, axis=-1).astype(jnp.bfloat16)  10.7 us
  transfers between devices with their start and end apart: 5, of which 4 were waited for; matrix products, arithmetic and copies ran while one was open for 18% of the time, Pallas kernels for 0%

commit v1 on v0

v1 whole, which is shorter than its diff:
```python
import functools

import jax
import jax.numpy as jnp
import numpy as np
from jax import lax
from jax.experimental import pallas as pl
from jax.experimental.pallas import tpu as pltpu
from jax.sharding import PartitionSpec as P

WIN = 12
HALF = 6
HEADS = 24
D = 768
CH = 512
HEIGHT = 768
WIDTH = 96
ROWS = 12
COLS = 24
TOK = ROWS * COLS
NW = WIN * WIN
EPS = 1e-5
F32 = jnp.float32
BF16 = jnp.bfloat16
HIGHEST = lax.Precision.HIGHEST
MESH = pl.DeviceIdType.MESH
VMEM = pl.BlockSpec(memory_space=pltpu.VMEM)
ANY = pl.BlockSpec(memory_space=pl.ANY)


def dot(a, b):
    return jnp.dot(a, b, preferred_element_type=F32)


def dot_exact(a, b):
    return jnp.dot(a, b, preferred_element_type=F32, precision=HIGHEST)


def hats(count, total):
    place = np.arange(total) + 0.5
    source = np.clip(place * count / total - 0.5, 0, count - 1)
    return np.maximum(0, 1 - np.abs(source[:, None] - np.arange(count)[None, :]))


def make_tables():
    t = {}
    perm_in = np.zeros((TOK, 384), np.float32)
    perm_out = np.zeros((320, TOK), np.float32)
    perm_fin = np.zeros((TOK, 320), np.float32)
    place = np.zeros((8, TOK), np.float32)
    for w in range(2):
        for p in range(WIN):
            for q in range(WIN):
                row, jj = w * NW + p * WIN + q, w * WIN + q
                low, edge = p >= HALF, jj >= COLS - HALF
                pp = p - HALF if low else p
                if not edge:
                    src = (NW if low else 0) + pp * COLS + HALF + jj
                    dst = (112 if low else 0) + pp * 18 + jj
                else:
                    src = 288 + (48 if low else 0) + pp * 8 + jj - 18
                    dst = 224 + (48 if low else 0) + pp * 6 + jj - 18
                perm_in[row, src] = 1
                perm_out[dst, row] = 1
                i = pp if low else pp + HALF
                j = jj - 18 if edge else jj + HALF
                perm_fin[i * COLS + j, dst] = 1
                place[0, row], place[1, row] = p, jj
    t["perm_in"], t["perm_out"], t["perm_fin"] = perm_in, perm_out, perm_fin
    t["place"] = place
    spot = np.zeros((TOK, 8), np.float32)
    spot[:, 0] = np.arange(TOK) // COLS
    spot[:, 1] = np.arange(TOK) % COLS
    t["spot"] = spot
    cells = np.full((48, 8), -9.0, np.float32)
    cells[:, 2] = 6
    for k in range(36):
        cells[k, :3] = (k // 6, k % 6, 6)
    for k in range(9):
        cells[36 + k, :3] = (k // 3, k % 3, 3)
    t["cells"] = cells
    t["cells_t"] = np.ascontiguousarray(cells.T)
    gather = np.zeros((96, 40), np.float32)
    inverse = np.zeros((96, 1), np.float32)
    mix = np.zeros((48, 96), np.float64)
    half_hat = np.array([[1, 1, 2 / 3, 1 / 3, 0, 0], [0, 0, 1 / 3, 2 / 3, 1, 1]])
    for scale, base in ((6, 0), (3, 48), (2, 64), (1, 80)):
        for a in range(scale):
            for b in range(scale):
                at = base + a * scale + b
                step = 6 // scale
                for u in range(step):
                    for v in range(step):
                        gather[at, (a * step + u) * 6 + b * step + v] = 1
                inverse[at] = (scale / HEIGHT) * (scale / WIDTH)
                if scale == 6:
                    mix[a * 6 + b, at] = 1
                elif scale == 3:
                    mix[36 + a * 3 + b, at] = 1
                elif scale == 2:
                    for m in range(6):
                        for n in range(6):
                            mix[m * 6 + n, at] = half_hat[a, m] * half_hat[b, n]
                else:
                    mix[:36, at] = 1
    t["gather"], t["inverse"], t["mix"] = gather, inverse, mix
    r6, c6, r3, c3 = hats(6, HEIGHT), hats(6, WIDTH), hats(3, HEIGHT), hats(3, WIDTH)
    rr = np.zeros((HEIGHT, 48))
    cc = np.zeros((WIDTH, 48))
    for k in range(36):
        rr[:, k], cc[:, k] = r6[:, k // 6], c6[:, k % 6]
    for k in range(9):
        rr[:, 36 + k], cc[:, 36 + k] = r3[:, k // 3], c3[:, k % 3]
    t["gram"] = (rr.T @ rr) * (cc.T @ cc)
    t["mass"] = (rr.sum(0) * cc.sum(0))[:, None]
    bf = ("perm_in", "perm_out", "perm_fin")
    return {k: np.asarray(v, BF16 if k in bf else np.float32) for k, v in t.items()}


def halo_kernel(tok, down, right, diag, send, recv):
    r, c = lax.axis_index("rows"), lax.axis_index("cols")
    nr, nc = lax.axis_size("rows"), lax.axis_size("cols")
    r_next, c_next = lax.rem(r + 1, nr), lax.rem(c + 1, nc)
    r_prev, c_prev = lax.rem(r + nr - 1, nr), lax.rem(c + nc - 1, nc)
    barrier = pltpu.get_barrier_semaphore()
    for to in ((r_next, c), (r, c_next), (r_next, c_next)):
        pl.semaphore_signal(barrier, inc=1, device_id=to, device_id_type=MESH)
    pl.semaphore_wait(barrier, 3)
    copies = []
    plan = (
        (tok.at[pl.ds(0, HALF)], down, (r_prev, c)),
        (tok.at[pl.ds(HALF, HALF), pl.ds(0, 8)], right, (r, c_prev)),
        (tok.at[pl.ds(0, HALF), pl.ds(0, 8)], diag, (r_prev, c_prev)),
    )
    for n, (src, dst, to) in enumerate(plan):
        copy = pltpu.make_async_remote_copy(
            src_ref=src, dst_ref=dst, send_sem=send.at[n], recv_sem=recv.at[n],
            device_id=to, device_id_type=MESH,
        )
        copy.start()
        copies.append(copy)
    for copy in copies:
        copy.wait()


def token_halo(tokens):
    return pl.pallas_call(
        halo_kernel,
        out_shape=(
            jax.ShapeDtypeStruct((HALF, COLS, D), BF16),
            jax.ShapeDtypeStruct((HALF, 8, D), BF16),
            jax.ShapeDtypeStruct((HALF, 8, D), BF16),
        ),
        in_specs=[ANY],
        out_specs=(ANY, ANY, ANY),
        scratch_shapes=[pltpu.SemaphoreType.DMA((3,)), pltpu.SemaphoreType.DMA((3,))],
        compiler_params=pltpu.CompilerParams(collective_id=0, has_side_effects=True),
        name="halo",
    )(tokens)


def block_kernel(
    tok, down, right, diag, perm_in, ln_gain, ln_bias, wqkv, bqkv, tab0, tab1, wproj, bproj,
    join, perm_out, place, cells, pay, moved, bias, bias_tail, qkv, xw, ctx, mask,
):
    r, c = lax.axis_index("rows"), lax.axis_index("cols")
    lane = lax.broadcasted_iota(jnp.int32, (HEADS, 384), 1)
    col = lax.rem(lane, WIN)
    for q in range(WIN):
        d = WIN - 1 - q
        base = tab0[...]
        if d:
            base = jnp.where(
                col < WIN - d,
                pltpu.roll(base, 384 - d, 1),
                pltpu.roll(tab1[...], WIN - d, 1),
            )
        for p in range(WIN):
            shift = (WIN - 1 - p) * WIN
            at = (p * WIN + q) * HEADS
            bias[at : at + HEADS, :] = base[:, shift : shift + 128]
            bias_tail[at : at + HEADS, :] = base[:, shift + 16 : shift + NW]

    iq = lax.broadcasted_iota(jnp.int32, (NW, NW), 0)
    ik = lax.broadcasted_iota(jnp.int32, (NW, NW), 1)
    row_cut = (iq >= NW // 2) != (ik >= NW // 2)
    col_cut = (lax.rem(iq, WIN) >= HALF) != (lax.rem(ik, WIN) >= HALF)
    last_row = jnp.where(r == lax.axis_size("rows") - 1, -100.0, 0.0).astype(F32)
    last_col = jnp.where(c == lax.axis_size("cols") - 1, -100.0, 0.0).astype(F32)
    by_row = jnp.where(row_cut, last_row, 0.0)
    mask[0] = by_row
    mask[1] = jnp.minimum(by_row, jnp.where(col_cut, last_col, 0.0))

    raw = jnp.concatenate([tok[NW : 2 * NW, :], down[...], right[...], diag[...]], 0)
    x = dot(perm_in[...], raw)
    xw[...] = x
    center = jnp.mean(x, -1, keepdims=True)
    cent = x - center
    spread = jnp.mean(cent * cent, -1, keepdims=True)
    normed = (cent * lax.rsqrt(spread + EPS) * ln_gain[...] + ln_bias[...]).astype(BF16)

    for n in range(9):
        part = slice(n * 256, (n + 1) * 256)
        acc = dot(normed, wqkv[:, part]) + bqkv[:, part]
        if n < 3:
            acc = acc * (32**-0.5)
        qkv[:, part] = acc.astype(BF16)

    lane_head = lax.broadcasted_iota(jnp.int32, (NW, 128), 1) // 32

    def group(g, carry):
        at = pl.multiple_of(g * 128, 128)
        for w in range(2):
            rows = pl.ds(w * NW, NW)
            qg = qkv[rows, pl.ds(at, 128)]
            kg = qkv[rows, pl.ds(pl.multiple_of(at + D, 128), 128)]
            vg = qkv[rows, pl.ds(pl.multiple_of(at + 2 * D, 128), 128)]
            out = jnp.zeros((NW, 128), F32)
            for h in range(4):
                qm = jnp.where(lane_head == h, qg, jnp.zeros_like(qg))
                s = lax.dot_general(qm, kg, (((1,), (1,)), ((), ())), preferred_element_type=F32)
                pick = pl.ds(g * 4 + h, NW, stride=HEADS)
                pair = jnp.concatenate([bias[pick, :], bias_tail[pick, :][:, 112:]], 1)
                s = s + pair + mask[w]
                e = jnp.exp(s - jnp.max(s, -1, keepdims=True))
                total = jnp.sum(e, -1, keepdims=True)
                o = dot(e.astype(BF16), vg) * (1.0 / total)
                out = jnp.where(lane_head == h, o, out)
            ctx[rows, pl.ds(at, 128)] = out.astype(BF16)
        return carry

    lax.fori_loop(0, 6, group, 0)

    block = (xw[...] + (dot(ctx[...], wproj[...]) + bproj[...])).astype(BF16)
    direct = dot(block, join[...])
    squares = jnp.sum(direct * direct, 0, keepdims=True)

    irow = place[0:1, :] + (r * ROWS + HALF).astype(F32)
    irow = jnp.where(irow >= HEIGHT, irow - HEIGHT, irow)
    icol = place[1:2, :] + (c * COLS + HALF).astype(F32)
    icol = jnp.where(icol >= WIDTH, icol - WIDTH, icol)
    ca, cb, cs = cells[:, 0:1], cells[:, 1:2], cells[:, 2:3]
    inside = (
        (irow >= ca[:40] * 128.0) & (irow < ca[:40] * 128.0 + 128.0)
        & (icol >= cb[:40] * 16.0) & (icol < cb[:40] * 16.0 + 16.0)
        & (cs[:40] > 4.0)
    )
    pooled = dot(jnp.where(inside, 1.0, 0.0).astype(BF16), block)
    row_at = jnp.clip((irow + 0.5) * (cs * (1.0 / HEIGHT)) - 0.5, 0.0, cs - 1.0)
    col_at = jnp.clip((icol + 0.5) * (cs * (1.0 / WIDTH)) - 0.5, 0.0, cs - 1.0)
    hat = jnp.maximum(1.0 - jnp.abs(row_at - ca), 0.0) * jnp.maximum(1.0 - jnp.abs(col_at - cb), 0.0)
    weighted = dot_exact(hat, direct)
    row_id = lax.broadcasted_iota(jnp.int32, (48, 1), 0)
    weighted = jnp.where(row_id == 45, squares, weighted)
    for n in range(6):
        pay[n * 40 : n * 40 + 40, :] = pooled[:, n * 128 : (n + 1) * 128]
    for n in range(4):
        pay[240 + n * 48 : 288 + n * 48, :] = weighted[:, n * 128 : (n + 1) * 128]
    pay[432:, :] = jnp.zeros((80, 128), F32)
    moved[...] = dot(perm_out[...], block).astype(BF16)


def reduce_kernel(pay, moved, full, halo, rs, zs, rs_send, rs_recv, z_send, z_recv, g_send, g_recv, h_send, h_recv):
    r, c = lax.axis_index("rows"), lax.axis_index("cols")
    nr, nc = lax.axis_size("rows"), lax.axis_size("cols")
    z = lax.rem(r // 4, 8)
    me = (r // 32) * 16 + lax.rem(r, 4) * 4 + c
    r_next, c_next = lax.rem(r + 1, nr), lax.rem(c + 1, nc)
    r_prev, c_prev = lax.rem(r + nr - 1, nr), lax.rem(c + nc - 1, nc)

    def plane(step):
        j = lax.rem(me + step, 32)
        return j, ((j // 16) * 32 + z * 4 + lax.rem(j // 4, 4), lax.rem(j, 4))

    def column(step):
        k = lax.rem(z + step, 8)
        return k, ((r // 32) * 32 + k * 4 + lax.rem(r, 4), c)

    barrier = pltpu.get_barrier_semaphore()

    def greet_plane(step, carry):
        _, to = plane(step)
        pl.semaphore_signal(barrier, inc=1, device_id=to, device_id_type=MESH)
        return carry

    def greet_column(step, carry):
        _, to = column(step)
        pl.semaphore_signal(barrier, inc=1, device_id=to, device_id_type=MESH)
        return carry

    lax.fori_loop(1, 8, greet_column, 0)
    lax.fori_loop(1, 32, greet_plane, 0)
    for to in ((r_prev, c), (r, c_prev), (r_prev, c_prev)):
        pl.semaphore_signal(barrier, inc=1, device_id=to, device_id_type=MESH)
    pl.semaphore_wait(barrier, 41)

    def remote(src, dst, s, v, to):
        return pltpu.make_async_remote_copy(
            src_ref=src, dst_ref=dst, send_sem=s, recv_sem=v, device_id=to, device_id_type=MESH
        )

    def rs_start(step, carry):
        j, to = plane(step)
        remote(pay.at[j], rs.at[me], rs_send, rs_recv, to).start()
        return carry

    lax.fori_loop(1, 32, rs_start, 0)
    halos = []
    for n, (src, dst, to) in enumerate(
        (
            (moved.at[pl.ds(112, 112)], halo.at[pl.ds(0, 112)], (r_next, c)),
            (moved.at[pl.ds(224, 48)], halo.at[pl.ds(112, 48)], (r, c_next)),
            (moved.at[pl.ds(272, 48)], halo.at[pl.ds(160, 48)], (r_next, c_next)),
        )
    ):
        copy = remote(src, dst, h_send.at[n], h_recv.at[n], to)
        copy.start()
        halos.append(copy)

    rs[me] = pay[me]
    remote(rs.at[pl.ds(0, 31)], rs.at[pl.ds(0, 31)], rs_send, rs_recv, (r_next, c)).wait_recv()
    zs[z] = jnp.sum(rs[...], 0)

    def z_start(step, carry):
        _, to = column(step)
        remote(zs.at[z], zs.at[z], z_send, z_recv, to).start()
        return carry

    lax.fori_loop(1, 8, z_start, 0)
    remote(zs.at[pl.ds(0, 7)], zs.at[pl.ds(0, 7)], z_send, z_recv, (r_next, c)).wait_recv()
    full[me] = jnp.sum(zs[...], 0)

    def g_start(step, carry):
        _, to = plane(step)
        remote(full.at[me], full.at[me], g_send, g_recv, to).start()
        return carry

    lax.fori_loop(1, 32, g_start, 0)
    remote(full.at[pl.ds(0, 31)], full.at[pl.ds(0, 31)], g_send, g_recv, (r_next, c)).wait_recv()
    for copy in halos:
        copy.wait()
    remote(rs.at[pl.ds(0, 31)], rs.at[pl.ds(0, 31)], rs_send, rs_recv, (r_next, c)).wait_send()
    remote(zs.at[pl.ds(0, 7)], zs.at[pl.ds(0, 7)], z_send, z_recv, (r_next, c)).wait_send()
    remote(full.at[pl.ds(0, 31)], full.at[pl.ds(0, 31)], g_send, g_recv, (r_next, c)).wait_send()


def reduce_all(pay, moved):
    dma = pltpu.SemaphoreType.DMA
    return pl.pallas_call(
        reduce_kernel,
        out_shape=(
            jax.ShapeDtypeStruct((32, 16, 128), F32),
            jax.ShapeDtypeStruct((208, D), BF16),
        ),
        in_specs=[VMEM, VMEM],
        out_specs=(VMEM, VMEM),
        scratch_shapes=[
            pltpu.VMEM((32, 16, 128), F32), pltpu.VMEM((8, 16, 128), F32),
            dma, dma, dma, dma, dma, dma, dma((3,)), dma((3,)),
        ],
        compiler_params=pltpu.CompilerParams(collective_id=1, has_side_effects=True),
        name="reduce",
    )(pay, moved)


def twice(values, weight):
    high = values.astype(BF16)
    low = (values - high.astype(F32)).astype(BF16)
    rows = values.shape[0]
    both = dot(jnp.concatenate([high, low], 0), weight)
    return both[:rows] + both[rows:]


def head_kernel(
    full, moved, halo, perm_fin, join, wbranch, bbranch, wjoin, bn_gain, bn_bias, gather, inverse,
    mix, gram, mass, spot, cells_t, out,
):
    r, c = lax.axis_index("rows"), lax.axis_index("cols")
    pooled = jnp.concatenate([full[n * 40 : n * 40 + 40, :] for n in range(6)], 1)
    weighted = jnp.concatenate([full[240 + n * 48 : 288 + n * 48, :] for n in range(4)], 1)
    means = dot_exact(gather[...], pooled) * inverse[...]
    parts = []
    for k, start, stop in ((3, 0, 48), (2, 48, 64), (1, 64, 80), (0, 80, 96)):
        hidden = twice(means[start:stop], wbranch[k]) + bbranch[k : k + 1, :]
        parts.append(twice(jnp.maximum(hidden, 0.0), wjoin[k]))
    lift = dot_exact(mix[...], jnp.concatenate(parts, 0))
    everyone = float(HEIGHT * WIDTH)
    total = jnp.sum(weighted[:36], 0, keepdims=True) + jnp.sum(mass[...] * lift, 0, keepdims=True)
    squares = (
        weighted[45:46]
        + 2.0 * jnp.sum(lift * weighted, 0, keepdims=True)
        + jnp.sum(lift * dot_exact(gram[...], lift), 0, keepdims=True)
    )
    mean_val = total * (1.0 / everyone)
    variance = squares * (1.0 / everyone) - mean_val * mean_val
    scale = bn_gain[...] * lax.rsqrt(variance + EPS)
    shift = bn_bias[...] - mean_val * scale
    x = dot(perm_fin[...], jnp.concatenate([moved[0:112, :], halo[...]], 0)).astype(BF16)
    direct = dot(x, join[...])
    irow = spot[:, 0:1] + (r * ROWS).astype(F32)
    icol = spot[:, 1:2] + (c * COLS).astype(F32)
    ca, cb, cs = cells_t[0:1, :], cells_t[1:2, :], cells_t[2:3, :]
    row_at = jnp.clip((irow + 0.5) * (cs * (1.0 / HEIGHT)) - 0.5, 0.0, cs - 1.0)
    col_at = jnp.clip((icol + 0.5) * (cs * (1.0 / WIDTH)) - 0.5, 0.0, cs - 1.0)
    hat = jnp.maximum(1.0 - jnp.abs(row_at - ca), 0.0) * jnp.maximum(1.0 - jnp.abs(col_at - cb), 0.0)
    pre = direct + dot_exact(hat, lift)
    out[...] = jnp.maximum(pre * scale + shift, 0.0).astype(BF16)


def shards(
    tokens, ln_gain, ln_bias, qkv_weight, qkv_bias, rel_table, proj_weight, proj_bias,
    branch_weight, branch_bias, join_block, join_branch, bn_gain, bn_bias,
):
    t = make_tables()
    down, right, diag = token_halo(tokens)
    table = rel_table[::-1, ::-1].transpose(2, 0, 1)
    tab0 = jnp.pad(table[:, :, :WIN].reshape(HEADS, 276), ((0, 0), (0, 108)))
    tab1 = jnp.pad(table[:, :, WIN:], ((0, 0), (0, 0), (0, 1))).reshape(HEADS, 276)
    tab1 = jnp.pad(tab1, ((0, 0), (0, 108)))
    pay, moved = pl.pallas_call(
        block_kernel,
        out_shape=(
            jax.ShapeDtypeStruct((512, 128), F32),
            jax.ShapeDtypeStruct((320, D), BF16),
        ),
        in_specs=[VMEM] * 17,
        out_specs=(VMEM, VMEM),
        scratch_shapes=[
            pltpu.VMEM((NW * HEADS, 128), F32),
            pltpu.VMEM((NW * HEADS, 128), F32),
            pltpu.VMEM((TOK, 3 * D), BF16),
            pltpu.VMEM((TOK, D), F32),
            pltpu.VMEM((TOK, D), BF16),
            pltpu.VMEM((2, NW, NW), F32),
        ],
        compiler_params=pltpu.CompilerParams(vmem_limit_bytes=40 * 2**20),
        name="block",
    )(
        tokens.reshape(TOK, D), down.reshape(NW, D), right.reshape(48, D), diag.reshape(48, D),
        t["perm_in"], ln_gain[None], ln_bias[None], qkv_weight, qkv_bias[None], tab0, tab1,
        proj_weight, proj_bias[None], join_block, t["perm_out"], t["place"], t["cells"],
    )
    full, halo = reduce_all(pay.reshape(32, 16, 128), moved)
    out = pl.pallas_call(
        head_kernel,
        out_shape=jax.ShapeDtypeStruct((TOK, CH), BF16),
        in_specs=[VMEM] * 17,
        out_specs=VMEM,
        compiler_params=pltpu.CompilerParams(vmem_limit_bytes=40 * 2**20),
        name="head",
    )(
        full.reshape(512, 128), moved, halo, t["perm_fin"], join_block, branch_weight, branch_bias,
        join_branch, bn_gain[None], bn_bias[None], t["gather"], t["inverse"], t["mix"], t["gram"],
        t["mass"], t["spot"], t["cells_t"],
    )
    return out.reshape(ROWS, COLS, CH)


def solution(mesh):
    in_specs = (P("rows", "cols", None),) + (P(),) * 13
    return jax.shard_map(
        shards, mesh=mesh, in_specs=in_specs, out_specs=P("rows", "cols", None), check_vma=False
    )
```

time: 456 us -> 99.8 us (0.22)
  waiting for transfers between devices: 178 us -> 0 us
  blocking collectives: 72.7 us -> 0 us
  Pallas kernels: 0 us -> 63.6 us
  matrix products: 54.9 us -> 0 us
  other arithmetic: 50.5 us -> 0 us
  local copies, waits for them, and re-layouts: 67.4 us -> 34.6 us
  starting transfers between devices: 14.5 us -> 0 us
  between operations: 14.1 us -> 0.14 us
    psum x1 -> x0, waiting for transfers between devices: 165 us -> none  [shards(): lax.psum((local_cells, local_weighted, jnp.sum(direct, axis=(0, 1)), jnp....]
    psum x1 -> x0, blocking collectives: 72.7 us -> none  [shards(): lax.psum((local_cells, local_weighted, jnp.sum(direct, axis=(0, 1)), jnp....]
    pallas_call x0 -> x4, Pallas kernels: none -> 63.6 us  [the longest x1 26.3 us: reduce_all(): pl.pallas_call(reduce_kernel, out_shape=(jax.ShapeDtypeStruct((32, 16, 12...]
    dot_general x41 -> x0, matrix products: 54.9 us -> none  [the longest x2 10.9 us: relative_bias(): jnp.einsum('pra,qsb,abh->hpqrs', onehot, onehot, rel_table, precision=hig...]
    add x3 -> x0, local copies, waits for them, and re-layouts: 28 us -> none  [the longest x2 25.6 us: window_attention(): scores = scores + pair_bias[None] + mask_add[:, None]]
    unnamed x82 -> x68, local copies, waits for them, and re-layouts: 1.56 us -> 28 us
    ppermute x4 -> x0, starting transfers between devices: 14.5 us -> none  [passed_along(): return lax.ppermute(value, axis, pairs)]
    transpose x3 -> x0, local copies, waits for them, and re-layouts: 13.2 us -> none  [the longest x1 12.3 us: relative_bias(): jnp.einsum('pra,qsb,abh->hpqrs', onehot, onehot, rel_table, precision=hig...]
  transfers between devices with their start and end apart: 5 -> 0, of which waited for: 4 -> 0; matrix products, arithmetic and copies ran while one was open for 18% -> 0% of each run, Pallas kernels for 0% -> 0%
where the time goes in v1:
time: 99.8 us; the launch traced here: 98.3 us
  Pallas kernels  63.6 us (64%)
  local copies, waits for them, and re-layouts  34.6 us (35%)
    unnamed x68, local copies, waits for them, and re-layouts  28 us
    pallas_call x1, Pallas kernels, reduce_all(): pl.pallas_call(reduce_kernel, out_shape=(jax.ShapeDtypeStruct((32, 16, 12...  26.3 us
    pallas_call x1, Pallas kernels, token_halo(): pl.pallas_call(halo_kernel, out_shape=(jax.ShapeDtypeStruct((HALF, COLS,...  18.5 us
    pallas_call x1, Pallas kernels, shards(): pl.pallas_call(block_kernel, out_shape=(jax.ShapeDtypeStruct((512, 128),...  15 us
    pallas_call x1, Pallas kernels, shards(): pl.pallas_call(head_kernel, out_shape=jax.ShapeDtypeStruct((TOK, CH), BF1...  3.84 us

profile of v1, /device:TPU:1, one launch (start us, length us, event | category | flops | bytes accessed | tf_op | source)
XLA Modules:
  0.0 98.3 jit_solution(459507729153513476)
XLA Ops:
  0.0 0.0 copy-start.12
  0.0 0.7 broadcast_in_dim.18.ln_gain
  0.7 1.3 %broadcast_in_dim.19.ln_bias = f32[1,768]{1,0:T(1,128)} reshape(f32[768]{0:T(1024)} %param.28) | data formatting | bytes 6144 | tf_op jit(solution)/shard_map/broadcast_in_dim | solution.py:440
  2.0 1.3 %broadcast_in_dim.21.bproj = f32[1,768]{1,0:T(1,128)} reshape(f32[768]{0:T(1024)} %param.33) | data formatting | bytes 6144 | tf_op jit(solution)/shard_map/broadcast_in_dim | solution.py:441
  3.3 0.7 broadcast_in_dim.20.bqkv
  4.0 1.0 %rev.3 = f32[23,23,24]{2,1,0:T(8,128)S(1)} reverse(f32[23,23,24]{2,1,0:T(8,128)} %param.31), dimensions={0,1} | reverse | bytes 101568 | tf_op jit(solution)/shard_map/rev | solution.py:416
  5.1 0.1 copy.31
  5.2 0.6 pad.11.tab0
  5.9 0.1 copy.32
  6.0 0.6 pad.13.tab1
  6.6 18.5 %halo.1 = (bf16[6,24,768]{2,1,0:T(8,128)(2,1)}, bf16[6,8,768]{2,1,0:T(8,128)(2,1)}, bf16[6,8,768]{2,1,0:T(8,128)(2,1)}) custom-call(bf16[12,24,768]{2,1,0:T(8,128)(2,1)} %tok.1), custom_call_target="tpu_custom_call" | custom-call | tf_op jit(solution)/shard_map/halo/pallas_call | solution.py:147
  25.1 0.0 copy-done.12
  25.1 0.0 copy-start
  25.1 2.0 %copy-done = bf16[768,2304]{1,0:T(8,128)(2,1)S(1)} copy-done((bf16[768,2304]{1,0:T(8,128)(2,1)S(1)}, bf16[768,2304]{1,0:T(8,128)(2,1)}, u32[]{:S(2)}) %copy-start) | copy-done | bytes 3538968
  27.1 0.0 copy-start.2
  27.1 1.1 %copy-done.2 = bf16[768,512]{1,0:T(8,128)(2,1)S(1)} copy-done((bf16[768,512]{1,0:T(8,128)(2,1)S(1)}, bf16[768,512]{1,0:T(8,128)(2,1)}, u32[]{:S(2)}) %copy-start.2) | copy-done | bytes 786456
  28.3 0.0 copy-start.7
  28.3 1.0 %copy-done.7 = bf16[12,24,768]{2,1,0:T(8,128)(2,1)S(1)} copy-done((bf16[12,24,768]{2,1,0:T(8,128)(2,1)S(1)}, bf16[12,24,768]{2,1,0:T(8,128)(2,1)}, u32[]{:S(2)}) %copy-start.7) | copy-done | bytes 442392
  29.3 0.0 copy-start.8
  29.3 1.3 %copy-done.8 = bf16[768,768]{1,0:T(8,128)(2,1)S(1)} copy-done((bf16[768,768]{1,0:T(8,128)(2,1)S(1)}, bf16[768,768]{1,0:T(8,128)(2,1)}, u32[]{:S(2)}) %copy-start.8) | copy-done | bytes 1179672
  30.5 0.0 copy-start.14
  30.5 0.9 copy-done.14
  31.5 0.0 copy-start.15
  31.5 0.9 copy-done.15
  32.4 0.0 copy-start.17
  32.4 0.8 copy-done.17
  33.2 0.0 copy-start.18
  33.2 0.8 copy-done.18
  33.9 0.0 copy-start.19
  33.9 0.9 copy-done.19
  34.8 0.0 copy-start.20
  34.8 0.9 copy-done.20
  35.7 0.0 copy-start.26
  35.7 0.7 copy-done.26
  36.5 0.0 copy-start.27
  36.5 0.7 copy-done.27
  37.1 0.0 copy-start.28
  37.1 0.7 copy-done.28
  37.8 0.0 copy-start.29
  37.8 0.7 copy-done.29
  38.5 15.0 %block.1 = (f32[512,128]{1,0:T(8,128)S(1)}, bf16[320,768]{1,0:T(8,128)(2,1)S(1)}) custom-call(bf16[288,768]{1,0:T(8,128)(2,1)S(1)} %bitcast.14, bf16[144,768]{1,0:T(8,128)(2,1)S(1)} %bitcast.17, bf16[48,768]{1,0:T(8,128)(2,1)S(1)} %bitcast.18, bf16[48,768]{1,0:T(8,128)(2,1)S(1)} %bitcast.19, bf16[288,384]{1,0:T(8,128)(2,1)S(1)} %copy-done.14, ...), custom_call_target="tpu_custom_call" | custom-call | tf_op jit(solution)/shard_map/block/pallas_call | solution.py:420
  53.5 0.0 copy-start.5
  53.5 0.8 copy-done.5
  54.3 0.7 copy-done.10
  55.0 26.3 %reduce.1 = (f32[32,16,128]{2,1,0:T(8,128)}, bf16[208,768]{1,0:T(8,128)(2,1)}) custom-call(f32[32,16,128]{2,1,0:T(8,128)} %bitcast.15, bf16[320,768]{1,0:T(8,128)(2,1)} %copy-done.5), custom_call_target="tpu_custom_call" | custom-call | tf_op jit(solution)/shard_map/reduce/pallas_call | solution.py:349
  81.3 0.0 copy-done.1
  81.3 0.0 copy-done.16
  81.3 0.0 copy-start.3
  81.3 1.1 %copy-done.3 = bf16[768,512]{1,0:T(8,128)(2,1)S(1)} copy-done((bf16[768,512]{1,0:T(8,128)(2,1)S(1)}, bf16[768,512]{1,0:T(8,128)(2,1)}, u32[]{:S(2)}) %copy-start.3) | copy-done | bytes 786456
  82.5 1.6 %copy-done.4 = bf16[4,512,512]{2,1,0:T(8,128)(2,1)S(1)} copy-done((bf16[4,512,512]{2,1,0:T(8,128)(2,1)S(1)}, bf16[4,512,512]{2,1,0:T(8,128)(2,1)}, u32[]{:S(2)}) %copy-start.4) | copy-done | bytes 2097176
  84.1 1.0 %copy-done.6 = bf16[320,768]{1,0:T(8,128)(2,1)S(1)} copy-done((bf16[320,768]{1,0:T(8,128)(2,1)S(1)}, bf16[320,768]{1,0:T(8,128)(2,1)}, u32[]{:S(2)}) %copy-start.6) | copy-done | bytes 491544
  85.1 1.0 copy-done.9
  86.1 0.9 copy-done.11
  87.0 0.9 copy-done.13
  88.0 0.8 copy-done.21
  88.7 0.8 copy-done.22
  89.5 0.7 copy-done.23
  90.3 0.7 copy-done.24
  91.0 0.7 copy-done.25
  91.8 0.7 copy-done.30
  92.5 0.7 copy-done.31
  93.1 0.7 copy-done.32
  93.8 0.7 copy-done.33
  94.5 3.8 %head.1 = bf16[288,512]{1,0:T(8,128)(2,1)} custom-call(f32[512,128]{1,0:T(8,128)S(1)} %bitcast.16, bf16[320,768]{1,0:T(8,128)(2,1)S(1)} %copy-done.6, bf16[208,768]{1,0:T(8,128)(2,1)S(1)} %copy-done.9, bf16[288,320]{1,0:T(8,128)(2,1)S(1)} %copy-done.13, bf16[768,512]{1,0:T(8,128)(2,1)S(1)} %copy-done.3, bf16[4,768,512]{2,1,0:T(8,128)(2,1)S(1)} %copy-done.1, ...), custom_call_target="tpu_custom_call" | custom-call | tf_op jit(solution)/shard_map/head/pallas_call | solution.py:444
  (22 shorter events, 0.1 us)
Async XLA Ops:
  0.0 25.1 %copy-start.12 = (bf16[320,288]{1,0:T(8,128)(2,1)S(1)}, bf16[320,288]{1,0:T(8,128)(2,1)}, u32[]{:S(2)}) copy-start(bf16[320,288]{1,0:T(8,128)(2,1)} %constant.28.clone.perm_out) | copy-start | bytes 552964
  25.1 2.0 %copy-start = (bf16[768,2304]{1,0:T(8,128)(2,1)S(1)}, bf16[768,2304]{1,0:T(8,128)(2,1)}, u32[]{:S(2)}) copy-start(bf16[768,2304]{1,0:T(8,128)(2,1)} %wqkv.1) | copy-start | bytes 10616836
  27.1 1.1 %copy-start.2 = (bf16[768,512]{1,0:T(8,128)(2,1)S(1)}, bf16[768,512]{1,0:T(8,128)(2,1)}, u32[]{:S(2)}) copy-start(bf16[768,512]{1,0:T(8,128)(2,1)} %join.3) | copy-start | bytes 2359300
  28.3 1.0 %copy-start.7 = (bf16[12,24,768]{2,1,0:T(8,128)(2,1)S(1)}, bf16[12,24,768]{2,1,0:T(8,128)(2,1)}, u32[]{:S(2)}) copy-start(bf16[12,24,768]{2,1,0:T(8,128)(2,1)} %tok.1) | copy-start | bytes 1327108
  29.3 1.3 %copy-start.8 = (bf16[768,768]{1,0:T(8,128)(2,1)S(1)}, bf16[768,768]{1,0:T(8,128)(2,1)}, u32[]{:S(2)}) copy-start(bf16[768,768]{1,0:T(8,128)(2,1)} %wproj.1) | copy-start | bytes 3538948
  30.5 0.9 copy-start.14
  31.5 0.9 copy-start.15
  32.4 0.8 copy-start.17
  33.2 0.8 copy-start.18
  33.9 0.9 copy-start.19
  34.8 0.9 copy-start.20
  35.7 0.7 copy-start.26
  36.5 0.7 copy-start.27
  37.1 0.7 copy-start.28
  37.8 0.7 copy-start.29
  38.5 42.8 %copy-start.1 = (bf16[4,768,512]{2,1,0:T(8,128)(2,1)S(1)}, bf16[4,768,512]{2,1,0:T(8,128)(2,1)}, u32[]{:S(2)}) copy-start(bf16[4,768,512]{2,1,0:T(8,128)(2,1)} %wbranch.1) | copy-start | bytes 9437188
  38.5 42.8 %copy-start.16 = (f32[288,8]{1,0:T(8,128)S(1)}, f32[288,8]{1,0:T(8,128)}, u32[]{:S(2)}) copy-start(f32[288,8]{1,0:T(8,128)} %constant.37.clone.spot) | copy-start | bytes 27652
  53.5 0.8 copy-start.5
  54.3 0.7 copy-start.10
  81.3 1.1 %copy-start.3 = (bf16[768,512]{1,0:T(8,128)(2,1)S(1)}, bf16[768,512]{1,0:T(8,128)(2,1)}, u32[]{:S(2)}) copy-start(bf16[768,512]{1,0:T(8,128)(2,1)} %join.3) | copy-start | bytes 2359300
  82.5 1.6 %copy-start.4 = (bf16[4,512,512]{2,1,0:T(8,128)(2,1)S(1)}, bf16[4,512,512]{2,1,0:T(8,128)(2,1)}, u32[]{:S(2)}) copy-start(bf16[4,512,512]{2,1,0:T(8,128)(2,1)} %wjoin.1) | copy-start | bytes 6291460
  84.1 1.0 %copy-start.6 = (bf16[320,768]{1,0:T(8,128)(2,1)S(1)}, bf16[320,768]{1,0:T(8,128)(2,1)}, u32[]{:S(2)}) copy-start(bf16[320,768]{1,0:T(8,128)(2,1)} %copy-done.5) | copy-start | bytes 1474564
  85.1 1.0 copy-start.9
  86.1 0.9 copy-start.11
  87.0 0.9 copy-start.13
  87.9 0.8 copy-start.21
  88.7 0.8 copy-start.22
  89.5 0.7 copy-start.23
  90.3 0.7 copy-start.24
  91.0 0.7 copy-start.25
  91.8 0.7 copy-start.30
  92.5 0.7 copy-start.31
  93.1 0.7 copy-start.32
  93.8 0.7 copy-start.33
